TPU v7x, 32 devices: a whole 2x2x4 slice. The times are simulated.
32 devices in a mesh: dp: 8 (over z, y), tensor: 4 (over x, core).
Axes of the slice: x: 2, y: 2, z: 4, core: 2. Of those that a mesh axis runs over, the one named last changes fastest.
Arguments:
- attn_out: bfloat16 [2048, 4096], P('dp', 'tensor'), may hold values from -6 to 6
- w_blocks: bfloat16 [4096, 8192], P('tensor', 'dp'), may hold values from -0.09375 to 0.09375
- w_scales: float32 [32, 8192], P('tensor', 'dp'), may hold values from 0.5 to 2
- residual: bfloat16 [2048, 8192], P('dp')
- gain: float32 [8192], P('tensor'), may hold values from 0.5 to 1.5
Outputs:
- hidden: bfloat16 [2048, 8192], P('dp', 'tensor')
- normed: bfloat16 [2048, 8192], P('dp', 'tensor')
All inputs are finite; a program needn't handle non-finite values.
Results may differ from a plain program's by a relative error of at most 0.014.
Values may be sent and summed in bfloat16 or wider, within the bound.
A program may use at most 128 MiB of HBM per device.

v0:
```python
import jax
import jax.numpy as jnp
from jax import lax
from jax.sharding import PartitionSpec as P

BLOCK = 128


def dequantize(blocks, scales):
    rows, cols = blocks.shape
    shaped = blocks.astype(jnp.float32).reshape(rows // BLOCK, BLOCK, cols)
    return (shaped * scales[:, None, :]).reshape(rows, cols).astype(jnp.bfloat16)


def on_device(attn_out, w_blocks, w_scales, residual, gain):
    everyone = lax.all_gather(attn_out, "dp", axis=0, tiled=True)
    local_cols = jnp.dot(
        everyone, dequantize(w_blocks, w_scales), preferred_element_type=jnp.float32
    )
    partial_value = lax.all_to_all(
        local_cols.astype(jnp.bfloat16), "dp", split_axis=0, concat_axis=1, tiled=True
    ).astype(local_cols.dtype)
    wide_cols = residual.shape[1]
    my_cols = gain.shape[0]
    offset = lax.axis_index("tensor") * my_cols
    total = lax.psum(partial_value.astype(jnp.bfloat16), "tensor").astype(jnp.float32)
    hidden_full = (residual.astype(jnp.float32) + total).astype(jnp.bfloat16)
    widened = hidden_full.astype(jnp.float32)
    mean_square = jnp.sum(widened * widened, axis=1, keepdims=True) / wide_cols
    mine = lax.dynamic_slice_in_dim(hidden_full, offset, my_cols, 1)
    normed = (mine.astype(jnp.float32) * gain[None, :] * lax.rsqrt(mean_square + 1e-05)).astype(
        jnp.bfloat16
    )
    return (mine, normed)


def solution(mesh):
    return jax.shard_map(
        on_device,
        mesh=mesh,
        in_specs=(
            P("dp", "tensor"),
            P("tensor", "dp"),
            P("tensor", "dp"),
            P("dp", None),
            P("tensor"),
        ),
        out_specs=(P("dp", "tensor"), P("dp", "tensor")),
        check_vma=False,
    )
```

profile of v0, /device:TPU:0, one launch (start us, length us, event | category | flops | bytes accessed | tf_op | source)
XLA Modules:
  0.0 293.9 jit_solution(12024145223568308483)
XLA Ops:
  7.2 0.0 all-gather.2.cloned.1.call-start
  7.2 0.7 all-gather.2.cloned.1.call-update
  7.9 0.0 all-reduce.2.cloned.1.call-start
  7.9 2.2 fusion
  10.1 75.5 %all-gather.2.cloned.1.call-done = bf16[2048,1024]{1,0:T(8,128)(2,1)} async-done(((bf16[256,1024]{1,0:T(8,128)(2,1)}), bf16[2048,1024]{1,0:T(8,128)(2,1)}) %all-gather.2.cloned.1.call-update) | async-done | bytes 4194320 | tf_op jit(solution)/shard_map/all_gather | solution.py:16
  85.6 7.0 %convolution_convert_fusion = bf16[1024,2048]{1,0:T(8,128)(2,1)S(1)} fusion(bf16[1024,1024]{1,0:T(8,128)(2,1)S(1)} %fusion, bf16[2048,1024]{1,0:T(8,128)(2,1)} %all-gather.2.cloned.1.call-done), kind=kOutput, calls=%fused_computation.5 | convolution fusion | flops 4297064448 | bytes 10485760 | tf_op jit(solution)/shard_map/dot_general | solution.py:17
  92.7 0.3 copy.12
  93.0 96.4 %all_to_all.19 = bf16[8,256,1024]{1,2,0:T(8,128)(2,1)} all-to-all(bf16[8,256,1024]{1,2,0:T(8,128)(2,1)S(1)} %bitcast.14), channel_id=1, replica_groups=mesh['dp'=8,'tensor'=4] {'dp'}, dimensions={0} | all-to-all | bytes 8388608 | tf_op jit(solution)/shard_map/all_to_all | solution.py:20
  189.4 6.4 %copy.9 = bf16[256,8192]{1,0:T(8,128)(2,1)} copy(bf16[256,8192]{0,1:T(8,128)(2,1)} %bitcast.15) | data formatting | bytes 8388608 | tf_op jit(solution)/shard_map/all_to_all | solution.py:20
  195.7 0.0 all-reduce.2.cloned.1.call-update
  195.8 0.0 copy-start
  195.8 84.3 %all-reduce.2.cloned.1.call-done = bf16[256,8192]{1,0:T(8,128)(2,1)} async-done(((bf16[256,8192]{1,0:T(8,128)(2,1)}), bf16[256,8192]{1,0:T(8,128)(2,1)}) %all-reduce.2.cloned.1.call-update) | async-done | bytes 4194320 | tf_op jit(solution)/shard_map/psum | solution.py:26
  280.1 5.4 %multiply_reduce_fusion = (f32[256]{0:T(256)S(1)}, bf16[256,8192]{1,0:T(8,128)(2,1)S(1)}) fusion(bf16[256,8192]{1,0:T(8,128)(2,1)} %all-reduce.2.cloned.1.call-done, bf16[256,8192]{1,0:T(8,128)(2,1)} %param.8), kind=kLoop, calls=%fused_computation | loop fusion | flops 14679808 | bytes 12583936 | tf_op jit(solution)/shard_map/reduce_sum | solution.py:29
  285.5 0.0 copy-done
  285.5 1.6 multiply_convert_fusion
  (1 shorter events, 0.0 us)
Async XLA Ops:
  7.2 78.5 %all-gather.2.cloned.1.call-start = ((), (), s32[]{:S(2)}) async-start(), calls=%async_computation.1 | async-start | bytes 4718592 | tf_op jit(solution)/shard_map/all_gather | solution.py:16
  7.9 272.2 %all-reduce.2.cloned.1.call-start = ((), (), s32[]{:S(2)}) async-start(), calls=%async_computation.2 | async-start | bytes 8388608 | tf_op jit(solution)/shard_map/psum | solution.py:26
  195.8 89.7 %copy-start = (f32[2048]{0:T(1024)S(1)}, f32[2048]{0:T(1024)}, u32[]{:S(2)}) copy-start(f32[2048]{0:T(1024)} %param.9) | copy-start | bytes 24580
Sparse Core Ops, SparseCore 0:
  10.1 75.5 all-gather.1
  195.9 84.1 all-reduce.1
where the time goes:
time: 294 us
  waiting for transfers between devices  161 us (55%)
  blocking collectives  96.4 us (33%)
  between operations  14.1 us (5%)
  other arithmetic  9.16 us (3%)
  matrix products  7.02 us (2%)
  local copies, waits for them, and re-layouts  6.65 us (2%)
    all_to_all x1, blocking collectives, on_device(): lax.all_to_all(local_cols.astype(jnp.bfloat16), 'dp', split_axis=0, conca...  96.4 us
    psum x1, waiting for transfers between devices, on_device(): lax.psum(partial_value.astype(jnp.bfloat16), 'tensor').astype(jnp.float32)  84.3 us
    all_gather x1, waiting for transfers between devices, on_device(): everyone = lax.all_gather(attn_out, 'dp', axis=0, tiled=True)  75.5 us
    dot_general x1, matrix products, on_device(): jnp.dot(everyone, dequantize(w_blocks, w_scales), preferred_element_type=...  7.02 us
    all_to_all x2, local copies, waits for them, and re-layouts, on_device(): lax.all_to_all(local_cols.astype(jnp.bfloat16), 'dp', split_axis=0, conca...  6.64 us
  transfers between devices with their start and end apart: 2, of which 2 were waited for; matrix products, arithmetic and copies ran while one was open for 1% of the time, Pallas kernels for 0%

commit v1 on v0

v1 whole, which is shorter than its diff:
```python
import functools

import jax
import jax.numpy as jnp
from jax import lax
from jax.experimental import pallas as pl
from jax.experimental.pallas import tpu as pltpu
from jax.sharding import PartitionSpec as P

MESH = pl.DeviceIdType.MESH
WIDTH = 256
LANES = 128


def plan(dp, groups, cols):
    inner = dp // groups
    width = min(WIDTH, cols)
    own = cols // width
    peers = (inner - 1) * own
    wave_of_seg = [0] * own + [1 + p * groups // peers for p in range(peers)]
    waves = [[] for _ in range(groups + 1)]
    for j in range(groups):
        for s, at in enumerate(wave_of_seg):
            waves[max(j, at)].append((j, s))
    return inner, width, own, wave_of_seg, waves


def kernel(
    dp, groups,
    a_ref, w_ref, sc_ref, res_hbm, gain_ref,
    hidden_ref, normed_ref,
    a_buf, w_buf, sc_buf, wd, res, part,
    snd1, rcv1, keep2, snd2, rcv2, snd3, zin, hs, acc, scl_snd, scl,
    res_sem, a_send, a_recv, w_send, w_recv, sc_send, sc_recv,
    s1, r1, s2, r2, s3, r3, s4, r4, s5, r5,
):
    rows, depth = a_ref.shape
    cols = w_ref.shape[1]
    my_cols = hidden_ref.shape[1]
    blocks = sc_ref.shape[0]
    per_block = depth // blocks
    half, quarter = rows // 2, rows // 4
    inner, width, own, wave_of_seg, waves = plan(dp, groups, cols)
    segs = len(wave_of_seg)

    d = lax.axis_index("dp")
    t = lax.axis_index("tensor")
    z, i = d // inner, d % inner
    core, x = t % 2, t // 2
    core_peer = t + 1 - 2 * core
    x_peer = (t + 2) % 4

    def line(o):
        return {"dp": o * inner + i, "tensor": t}

    def row(other):
        return {"dp": d, "tensor": other}

    def pair(other):
        return {"dp": z * inner + other, "tensor": t}

    def step_block(j):
        if j == 0:
            return z
        if j == 1:
            return z + 1 - 2 * (z % 2)
        if j == 2:
            return z + 2 - 4 * (z // 2)
        return 3 - z

    def row_offset(who):
        return pl.multiple_of((who % 2) * half + (who // 2) * quarter, quarter)

    def seg_col(s):
        return pl.multiple_of(((i + s // own) % inner) * cols + (s % own) * width, width)

    def remote(src, dst, send, recv, to):
        return pltpu.make_async_remote_copy(
            src_ref=src, dst_ref=dst, send_sem=send, recv_sem=recv,
            device_id=to, device_id_type=MESH,
        )

    mine = row_offset(t)
    res_copy = pltpu.make_async_copy(res_hbm.at[pl.ds(mine, quarter), :], res, res_sem)
    res_copy.start()

    barrier = pltpu.get_barrier_semaphore()
    for r in range(1, inner):
        pl.semaphore_signal(barrier, inc=1, device_id=pair((i + r) % inner), device_id_type=MESH)
    for r in range(1, groups):
        pl.semaphore_signal(barrier, inc=1, device_id=line((z + r) % groups), device_id_type=MESH)
    for r in range(1, 4):
        pl.semaphore_signal(barrier, inc=1, device_id=row((t + r) % 4), device_id_type=MESH)
    pl.semaphore_wait(barrier, inner - 1 + groups - 1 + 3)

    def a_copy(src, block, send, to):
        return remote(src, a_buf.at[block], a_send.at[send], a_recv.at[block], line(to))

    @pl.when(z < groups - 1)
    def _():
        a_copy(a_ref, z, z, z + 1).start()

    @pl.when(z > 0)
    def _():
        a_copy(a_ref, z, groups, z - 1).start()

    def sc_copy(r):
        return remote(sc_ref, sc_buf.at[r - 1], sc_send.at[r - 1], sc_recv.at[r - 1], pair((i + inner - r) % inner))

    def w_copy(r, c):
        k = (r - 1) * own + c
        return remote(
            w_ref.at[:, pl.ds(c * width, width)], w_buf.at[k], w_send.at[k], w_recv.at[k],
            pair((i + inner - r) % inner),
        )

    for r in range(1, inner):
        sc_copy(r).start()
    for r in range(1, inner):
        for c in range(own):
            w_copy(r, c).start()

    def dequantize(s):
        c = s % own
        for b in range(blocks):
            lines = pl.ds(b * per_block, per_block)
            if s < own:
                raw = w_ref[lines, pl.ds(c * width, width)]
                scale = sc_ref[pl.ds(b, 1), pl.ds(c * width, width)]
            else:
                raw = w_buf[s - own, lines, :]
                scale = sc_buf[s // own - 1, pl.ds(b, 1), pl.ds(c * width, width)]
            wd[s, lines, :] = (raw.astype(jnp.float32) * scale).astype(jnp.bfloat16)

    def forward(k):
        @pl.when(z >= k)
        def _():
            b = z - k
            a_copy(a_ref, b, b, z).wait_recv()

            @pl.when(z < groups - 1)
            def _():
                a_copy(a_buf.at[b], b, b, z + 1).start()

        @pl.when(z + k <= groups - 1)
        def _():
            b = z + k
            a_copy(a_ref, b, b, z).wait_recv()

            @pl.when(z > 0)
            def _():
                a_copy(a_buf.at[b], b, b, z - 1).start()

    def copy1(u):
        return remote(snd1.at[u], rcv1.at[u], s1.at[u], r1.at[u], row(core_peer))

    def copy2(u):
        return remote(snd2.at[u], rcv2.at[u], s2.at[u], r2.at[u], row(x_peer))

    def copy3(u, j):
        return remote(snd3.at[u], zin.at[u], s3.at[u], r3.at[u], line(step_block(j)))

    def copy4(u, j, s):
        return remote(
            hs.at[u], hidden_ref.at[pl.ds(mine, quarter), pl.ds(seg_col(s), width)],
            s4.at[u], r4.at[t * segs + s], row(step_block(j)),
        )

    keep_rows = pl.multiple_of(core * half, half)
    send_rows = pl.multiple_of((1 - core) * half, half)

    def stage1(u, j, s):
        a = a_ref[...] if j == 0 else a_buf[step_block(j)]
        part[u % 2] = jnp.dot(a, wd[s], preferred_element_type=jnp.float32)
        snd1[u] = part[u % 2, pl.ds(send_rows, half), :].astype(jnp.bfloat16)
        copy1(u).start()

    def stage2(u):
        copy1(u).wait_recv()
        near = pl.multiple_of(x * quarter, quarter)
        far = pl.multiple_of((1 - x) * quarter, quarter)
        snd2[u] = (
            part[u % 2, pl.ds(pl.multiple_of(keep_rows + far, quarter), quarter), :]
            + rcv1[u, pl.ds(far, quarter), :].astype(jnp.float32)
        ).astype(jnp.bfloat16)
        copy2(u).start()
        keep2[u] = (
            part[u % 2, pl.ds(pl.multiple_of(keep_rows + near, quarter), quarter), :]
            + rcv1[u, pl.ds(near, quarter), :].astype(jnp.float32)
        )

    def stage3(u, j):
        copy2(u).wait_recv()
        total = (keep2[u] + rcv2[u].astype(jnp.float32)).astype(jnp.bfloat16)
        if j == 0:
            zin[u] = total
        else:
            snd3[u] = total
            copy3(u, j).start()

    def stage4(u, j, s):
        if j > 0:
            copy3(u, j).wait_recv()
        source = step_block(j)
        at = pl.multiple_of(source * my_cols + seg_col(s), width)
        h = (zin[u].astype(jnp.float32) + res[:, pl.ds(at, width)].astype(jnp.float32)).astype(jnp.bfloat16)
        hs[u] = h

        @pl.when(source != t)
        def _():
            copy4(u, j, s).start()

        @pl.when(source == t)
        def _():
            hidden_ref[pl.ds(mine, quarter), pl.ds(seg_col(s), width)] = hs[u]

        wide = h.astype(jnp.float32)
        square = wide * wide
        total = acc[...]
        for k in range(width // LANES):
            total = total + square[:, k * LANES:(k + 1) * LANES]
        acc[...] = total

    acc[...] = jnp.zeros_like(acc)
    number = 0
    late = []
    units = []
    for w, wave in enumerate(waves):
        if 1 <= w < groups:
            forward(w)
        for s in range(segs):
            if wave_of_seg[s] == w:
                if s >= own:
                    r, c = s // own, s % own
                    if c == 0:
                        sc_copy(r).wait_recv()
                    w_copy(r, c).wait_recv()
                dequantize(s)
        now = [(number + k, j, s) for k, (j, s) in enumerate(wave)]
        number += len(wave)
        for k, (u, j, s) in enumerate(now):
            stage1(u, j, s)
            if k > 0:
                stage2(now[k - 1][0])
        if now:
            stage2(now[-1][0])
        if w == 1:
            res_copy.wait()
        for u, j, s in late:
            stage4(u, j, s)
        for u, j, s in now:
            stage3(u, j)
        late = now
        units += now
    for u, j, s in late:
        stage4(u, j, s)

    mean_square = jnp.sum(acc[...], axis=1, keepdims=True) / (my_cols * groups)
    scl_snd[...] = jnp.broadcast_to(lax.rsqrt(mean_square + 1e-05), scl_snd.shape)
    scl[pl.ds(mine, quarter), :] = scl_snd[...]

    def copy5(r):
        return remote(
            scl_snd, scl.at[pl.ds(mine, quarter), :], s5.at[r - 1], r5.at[t], row((t + r) % 4)
        )

    for r in range(1, 4):
        copy5(r).start()

    def normalize(who):
        at = pl.ds(row_offset(who), quarter)
        scale = scl[at, :]
        for k in range(my_cols // LANES):
            lanes = pl.ds(k * LANES, LANES)
            normed_ref[at, lanes] = (
                hidden_ref[at, lanes].astype(jnp.float32) * gain_ref[:, lanes] * scale
            ).astype(jnp.bfloat16)

    normalize(t)
    for r in range(1, 4):
        who = (t + r) % 4
        at = pl.ds(row_offset(who), quarter)
        for s in range(segs):
            piece = hidden_ref.at[at, pl.ds(seg_col(s), width)]
            remote(hs.at[0], piece, s4.at[0], r4.at[who * segs + s], row(who)).wait_recv()
        remote(scl_snd, scl.at[at, :], s5.at[0], r5.at[who], row(who)).wait_recv()
        normalize(who)

    @pl.when(z < groups - 1)
    def _():
        a_copy(a_ref, z, z, z + 1).wait_send()

    @pl.when(z > 0)
    def _():
        a_copy(a_ref, z, groups, z - 1).wait_send()

    for k in range(1, groups):
        @pl.when((z >= k) & (z < groups - 1))
        def _():
            a_copy(a_ref, z - k, z - k, z + 1).wait_send()

        @pl.when((z + k <= groups - 1) & (z > 0))
        def _():
            a_copy(a_ref, z + k, z + k, z - 1).wait_send()

    for r in range(1, inner):
        sc_copy(r).wait_send()
        for c in range(own):
            w_copy(r, c).wait_send()
    for u, j, s in units:
        copy1(u).wait_send()
        copy2(u).wait_send()
        if j > 0:
            copy3(u, j).wait_send()

        @pl.when(step_block(j) != t)
        def _():
            copy4(u, j, s).wait_send()
    for r in range(1, 4):
        copy5(r).wait_send()


def solution(mesh):
    dp, groups = mesh.shape["dp"], mesh.shape["tensor"]

    def on_device(attn_out, w_blocks, w_scales, residual, gain):
        rows, depth = attn_out.shape
        cols = w_blocks.shape[1]
        my_cols = gain.shape[0]
        inner, width, own, wave_of_seg, waves = plan(dp, groups, cols)
        segs = len(wave_of_seg)
        n = segs * groups
        peers = segs - own
        half, quarter = rows // 2, rows // 4
        bf16, f32 = jnp.bfloat16, jnp.float32
        vmem = pl.BlockSpec(memory_space=pltpu.VMEM)
        dma = pltpu.SemaphoreType.DMA
        out = jax.ShapeDtypeStruct((rows, my_cols), bf16)
        return tuple(pl.pallas_call(
            functools.partial(kernel, dp, groups),
            out_shape=(out, out),
            in_specs=[vmem, vmem, vmem, pl.BlockSpec(memory_space=pl.ANY), vmem],
            out_specs=(vmem, vmem),
            scratch_shapes=[
                pltpu.VMEM((groups, rows, depth), bf16),
                pltpu.VMEM((peers, depth, width), bf16),
                pltpu.VMEM((inner - 1,) + w_scales.shape, f32),
                pltpu.VMEM((segs, depth, width), bf16),
                pltpu.VMEM((quarter, residual.shape[1]), bf16),
                pltpu.VMEM((2, rows, width), f32),
                pltpu.VMEM((n, half, width), bf16),
                pltpu.VMEM((n, half, width), bf16),
                pltpu.VMEM((n, quarter, width), f32),
                pltpu.VMEM((n, quarter, width), bf16),
                pltpu.VMEM((n, quarter, width), bf16),
                pltpu.VMEM((n, quarter, width), bf16),
                pltpu.VMEM((n, quarter, width), bf16),
                pltpu.VMEM((n, quarter, width), bf16),
                pltpu.VMEM((quarter, LANES), f32),
                pltpu.VMEM((quarter, LANES), f32),
                pltpu.VMEM((rows, LANES), f32),
                dma, dma((groups + 1,)), dma((groups,)), dma((peers,)), dma((peers,)),
                dma((inner - 1,)), dma((inner - 1,)),
                dma((n,)), dma((n,)), dma((n,)), dma((n,)), dma((n,)), dma((n,)),
                dma((n,)), dma((groups * segs,)), dma((3,)), dma((groups,)),
            ],
            compiler_params=pltpu.CompilerParams(
                collective_id=0, has_side_effects=True, vmem_limit_bytes=60 * 1024 * 1024,
            ),
        )(attn_out, w_blocks, w_scales, residual, gain.reshape(1, my_cols)))

    return jax.shard_map(
        on_device,
        mesh=mesh,
        in_specs=(
            P("dp", "tensor"),
            P("tensor", "dp"),
            P("tensor", "dp"),
            P("dp", None),
            P("tensor"),
        ),
        out_specs=(P("dp", "tensor"), P("dp", "tensor")),
        check_vma=False,
    )
```

time: 294 us -> 86.3 us (0.29)
  waiting for transfers between devices: 161 us -> 0 us
  blocking collectives: 96.4 us -> 0 us
  Pallas kernels: 0 us -> 80.9 us
  between operations: 14.1 us -> 0.64 us
  other arithmetic: 9.16 us -> 0 us
  matrix products: 7.02 us -> 0 us
    all_to_all x1 -> x0, blocking collectives: 96.4 us -> none  [on_device(): lax.all_to_all(local_cols.astype(jnp.bfloat16), 'dp', split_axis=0, conca...]
    psum x1 -> x0, waiting for transfers between devices: 84.3 us -> none  [on_device(): lax.psum(partial_value.astype(jnp.bfloat16), 'tensor').astype(jnp.float32)]
    pallas_call x0 -> x1, Pallas kernels: none -> 80.9 us  [on_device(): pl.pallas_call(functools.partial(kernel, dp, groups), out_shape=(out, out...]
    all_gather x1 -> x0, waiting for transfers between devices: 75.5 us -> none  [on_device(): everyone = lax.all_gather(attn_out, 'dp', axis=0, tiled=True)]
    dot_general x1 -> x0, matrix products: 7.02 us -> none  [on_device(): jnp.dot(everyone, dequantize(w_blocks, w_scales), preferred_element_type=...]
    all_to_all x2 -> x0, local copies, waits for them, and re-layouts: 6.64 us -> none  [on_device(): lax.all_to_all(local_cols.astype(jnp.bfloat16), 'dp', split_axis=0, conca...]
    reduce_sum x1 -> x0, other arithmetic: 5.4 us -> none  [on_device(): mean_square = jnp.sum(widened * widened, axis=1, keepdims=True) / wide_cols]
    unnamed x2, local copies, waits for them, and re-layouts: 0.01 us -> 4.61 us
  transfers between devices with their start and end apart: 2 -> 0, of which waited for: 2 -> 0; matrix products, arithmetic and copies ran while one was open for 1% -> 0% of each run, Pallas kernels for 0% -> 0%
where the time goes in v1:
time: 86.3 us; the launch traced here: 86.1 us
  Pallas kernels  80.9 us (94%)
  local copies, waits for them, and re-layouts  4.61 us (5%)
    pallas_call x1, Pallas kernels, on_device(): pl.pallas_call(functools.partial(kernel, dp, groups), out_shape=(out, out...  80.9 us
    unnamed x2, local copies, waits for them, and re-layouts  4.61 us

profile of v1, /device:TPU:0, one launch (start us, length us, event | category | flops | bytes accessed | tf_op | source)
XLA Modules:
  0.0 86.1 jit_solution(1756569253155000265)
XLA Ops:
  0.6 80.9 %shard_map.68 = (bf16[256,2048]{1,0:T(8,128)(2,1)}, bf16[256,2048]{1,0:T(8,128)(2,1)}) custom-call(bf16[256,1024]{1,0:T(8,128)(2,1)} %a_ref.1, bf16[1024,1024]{1,0:T(8,128)(2,1)} %w_ref.1, f32[8,1024]{1,0:T(8,128)} %sc_ref.1, bf16[256,8192]{1,0:T(8,128)(2,1)} %res_hbm.1, f32[1,2048]{1,0:T(1,128)} %bitcast.1), custom_call_target="tpu_custom_call" | custom-call | tf_op jit(solution)/shard_map/pallas_call | solution.py:339
  81.5 2.3 %copy.9 = bf16[256,2048]{1,0:T(8,128)(2,1)} copy(bf16[256,2048]{1,0:T(8,128)(2,1)} %get-tuple-element.4) | data formatting | bytes 2097152
  83.8 2.3 %copy.10 = bf16[256,2048]{1,0:T(8,128)(2,1)} copy(bf16[256,2048]{1,0:T(8,128)(2,1)} %get-tuple-element.5) | data formatting | bytes 2097152

commit v2 on v1

--- a/solution.py
+++ b/solution.py
@@ -27,10 +27,10 @@
 
 def kernel(
     dp, groups,
-    a_ref, w_ref, sc_ref, res_hbm, gain_ref,
-    hidden_ref, normed_ref,
+    a_ref, w_ref, sc_ref, res_hbm,
+    hidden_ref, scl,
     a_buf, w_buf, sc_buf, wd, res, part,
-    snd1, rcv1, keep2, snd2, rcv2, snd3, zin, hs, acc, scl_snd, scl,
+    snd1, rcv1, keep2, snd2, rcv2, snd3, zin, hs, acc, scl_snd,
     res_sem, a_send, a_recv, w_send, w_recv, sc_send, sc_recv,
     s1, r1, s2, r2, s3, r3, s4, r4, s5, r5,
 ):
@@ -267,16 +267,6 @@
     for r in range(1, 4):
         copy5(r).start()
 
-    def normalize(who):
-        at = pl.ds(row_offset(who), quarter)
-        scale = scl[at, :]
-        for k in range(my_cols // LANES):
-            lanes = pl.ds(k * LANES, LANES)
-            normed_ref[at, lanes] = (
-                hidden_ref[at, lanes].astype(jnp.float32) * gain_ref[:, lanes] * scale
-            ).astype(jnp.bfloat16)
-
-    normalize(t)
     for r in range(1, 4):
         who = (t + r) % 4
         at = pl.ds(row_offset(who), quarter)
@@ -284,7 +274,6 @@
             piece = hidden_ref.at[at, pl.ds(seg_col(s), width)]
             remote(hs.at[0], piece, s4.at[0], r4.at[who * segs + s], row(who)).wait_recv()
         remote(scl_snd, scl.at[at, :], s5.at[0], r5.at[who], row(who)).wait_recv()
-        normalize(who)
 
     @pl.when(z < groups - 1)
     def _():
@@ -336,10 +325,10 @@
         vmem = pl.BlockSpec(memory_space=pltpu.VMEM)
         dma = pltpu.SemaphoreType.DMA
         out = jax.ShapeDtypeStruct((rows, my_cols), bf16)
-        return tuple(pl.pallas_call(
+        hidden, scale = pl.pallas_call(
             functools.partial(kernel, dp, groups),
-            out_shape=(out, out),
-            in_specs=[vmem, vmem, vmem, pl.BlockSpec(memory_space=pl.ANY), vmem],
+            out_shape=(out, jax.ShapeDtypeStruct((rows, LANES), f32)),
+            in_specs=[vmem, vmem, vmem, pl.BlockSpec(memory_space=pl.ANY)],
             out_specs=(vmem, vmem),
             scratch_shapes=[
                 pltpu.VMEM((groups, rows, depth), bf16),
@@ -358,7 +347,6 @@
                 pltpu.VMEM((n, quarter, width), bf16),
                 pltpu.VMEM((quarter, LANES), f32),
                 pltpu.VMEM((quarter, LANES), f32),
-                pltpu.VMEM((rows, LANES), f32),
                 dma, dma((groups + 1,)), dma((groups,)), dma((peers,)), dma((peers,)),
                 dma((inner - 1,)), dma((inner - 1,)),
                 dma((n,)), dma((n,)), dma((n,)), dma((n,)), dma((n,)), dma((n,)),
@@ -367,7 +355,9 @@
             compiler_params=pltpu.CompilerParams(
                 collective_id=0, has_side_effects=True, vmem_limit_bytes=60 * 1024 * 1024,
             ),
-        )(attn_out, w_blocks, w_scales, residual, gain.reshape(1, my_cols)))
+        )(attn_out, w_blocks, w_scales, residual)
+        normed = (hidden.astype(f32) * gain[None, :] * scale[:, :1]).astype(bf16)
+        return hidden, normed
 
     return jax.shard_map(
         on_device,

time: 86.3 us -> 85.8 us (level)
  local copies, waits for them, and re-layouts: 4.61 us -> 2.07 us
  other arithmetic: 0 us -> 2.46 us
    unnamed x2 -> x5, local copies, waits for them, and re-layouts: 4.61 us -> 0.98 us
    convert_element_type x0 -> x1, other arithmetic: none -> 2.46 us  [on_device(): normed = (hidden.astype(f32) * gain[None, :] * scale[:, :1]).astype(bf16)]
    slice x0 -> x1, local copies, waits for them, and re-layouts: none -> 1.09 us  [on_device(): normed = (hidden.astype(f32) * gain[None, :] * scale[:, :1]).astype(bf16)]
where the time goes in v2:
time: 85.8 us; the launch traced here: 85.6 us
  Pallas kernels  80.4 us (94%)
  other arithmetic  2.46 us (3%)
  local copies, waits for them, and re-layouts  2.07 us (2%)
    pallas_call x1, Pallas kernels, on_device(): pl.pallas_call(functools.partial(kernel, dp, groups), out_shape=(out, jax...  80.4 us
    convert_element_type x1, other arithmetic, on_device(): normed = (hidden.astype(f32) * gain[None, :] * scale[:, :1]).astype(bf16)  2.46 us

profile of v2, /device:TPU:0, one launch (start us, length us, event | category | flops | bytes accessed | tf_op | source)
XLA Modules:
  0.0 85.6 jit_solution(17127581259740803568)
XLA Ops:
  0.6 0.0 copy-start.1
  0.6 80.4 %shard_map.68 = (bf16[256,2048]{1,0:T(8,128)(2,1)}, f32[256,128]{1,0:T(8,128)}) custom-call(bf16[256,1024]{1,0:T(8,128)(2,1)} %a_ref.1, bf16[1024,1024]{1,0:T(8,128)(2,1)} %w_ref.1, f32[8,1024]{1,0:T(8,128)} %sc_ref.1, bf16[256,8192]{1,0:T(8,128)(2,1)} %res_hbm.1), custom_call_target="tpu_custom_call" | custom-call | tf_op jit(solution)/shard_map/pallas_call | solution.py:328
  81.0 0.0 copy-start
  81.0 1.1 %slice_reduce_fusion = f32[256]{0:T(256)S(1)} fusion(f32[256,128]{1,0:T(8,128)} %get-tuple-element.5), kind=kLoop, calls=%fused_computation.1 | loop fusion | bytes 2048 | tf_op jit(solution)/shard_map/slice | solution.py:359
  82.1 0.0 copy-done.1
  82.1 2.5 %multiply_convert_fusion = bf16[256,2048]{1,0:T(8,128)(2,1)} fusion(bf16[256,2048]{1,0:T(8,128)(2,1)} %get-tuple-element.8, f32[256]{0:T(256)S(1)} %slice_reduce_fusion, f32[2048]{0:T(1024)S(1)} %copy-done.1), kind=kLoop, calls=%fused_computation | loop fusion | flops 2097152 | bytes 2106368 | tf_op jit(solution)/shard_map/convert_element_type | solution.py:359
  84.6 0.0 copy-done
  84.6 1.0 %copy.8 = bf16[256,2048]{1,0:T(8,128)(2,1)} copy(bf16[256,2048]{1,0:T(8,128)(2,1)S(1)} %copy-done) | data formatting | bytes 2097152
Async XLA Ops:
  0.6 81.5 %copy-start.1 = (f32[2048]{0:T(1024)S(1)}, f32[2048]{0:T(1024)}, u32[]{:S(2)}) copy-start(f32[2048]{0:T(1024)} %param.9) | copy-start | bytes 24580
  81.0 3.6 %copy-start = (bf16[256,2048]{1,0:T(8,128)(2,1)S(1)}, bf16[256,2048]{1,0:T(8,128)(2,1)}, u32[]{:S(2)}) copy-start(bf16[256,2048]{1,0:T(8,128)(2,1)} %get-tuple-element.8) | copy-start | bytes 3145732
